TPU v7x, 32 devices: a whole 2x2x4 slice. The times are simulated.
32 devices in a mesh: pw: 8 (over z, core), band: 4 (over y, x).
Axes of the slice: x: 2, y: 2, z: 4, core: 2. Of those that a mesh axis runs over, the one named last changes fastest.
Arguments:
- wavefunctions: bfloat16 [2, 4096, 512], P(None, 'pw', 'band'), may hold values from -0.09375 to 0.09375
- miller: int32 [3, 4096], P(None, 'pw'), may hold values from -16 to 16
- reciprocal: float32 [3, 3], replicated, may hold values from -0.15 to 1.15, as said below
- fractional: float32 [3, 32], replicated, may hold values from 0 to 1
- species: int32 [32], replicated, may hold values from 0 to 3
- atom_order: int32 [32], replicated, may hold values from 0 to 31, each once
- radial_widths: float32 [4, 4], replicated, may hold values from 0.003 to 0.02
- onsite_base: float32 [4, 8, 8], replicated, may hold values from -2 to 2
- coupling: float32 [4, 64, 64], replicated, may hold values from -0.75 to 0.75
- occupations: float32 [512], P('band'), may hold values from 0 to 3, as said below
Outputs:
- applied: bfloat16 [2, 4096, 512], P(None, 'pw', 'band')
- onsite_d: float32 [32, 8, 8], P('pw')
Inputs may be any that keep to these rules, and one draw needn't show every extreme that they name: `atom_order`: a permutation of the atoms. `reciprocal`: each diagonal entry is 0.85 or more and each other entry 0.15 or less in magnitude. `occupations`: positive.
All inputs are finite; a program needn't handle non-finite values.
Results may differ from a plain program's by a relative error of at most 0.008.
Values may be sent and summed in bfloat16 or wider, within the bound.
A program may use at most 64 MiB of HBM per device.

v0:
```python
import math
import jax
import jax.numpy as jnp
from jax import lax
from jax.sharding import PartitionSpec as P

HIGH = lax.Precision.HIGHEST


def projector_tile(miller_cols, reciprocal, positions, atom_species, radial_widths):
    two_pi = 2.0 * math.pi
    miller_real = miller_cols.astype(jnp.float32)
    g_vectors = two_pi * jnp.dot(reciprocal, miller_real, precision=HIGH)
    g_square = jnp.sum(g_vectors * g_vectors, axis=0)
    phases = two_pi * jnp.dot(positions.T, miller_real, precision=HIGH)
    onehot = (
        atom_species[:, None] == jnp.arange(radial_widths.shape[0], dtype=jnp.int32)[None, :]
    ).astype(jnp.float32)
    widths = jnp.dot(onehot, radial_widths, precision=HIGH)
    radial = jnp.exp(-0.5 * g_square[None, None, :] * (widths * widths)[:, :, None])
    s_part = radial[:, 0:2, :]
    p_first = g_vectors[None, :, :] * (widths[:, 2, None, None] * radial[:, 2:3, :])
    p_second = g_vectors[None, :, :] * (widths[:, 3, None, None] * radial[:, 3:4, :])
    p_part = jnp.concatenate([p_first, p_second], axis=1)
    cosine = jnp.cos(phases)[:, None, :]
    sine = jnp.sin(phases)[:, None, :]
    beta_real = jnp.concatenate([s_part * cosine, -p_part * sine], axis=1)
    beta_imag = jnp.concatenate([-s_part * sine, -p_part * cosine], axis=1)
    rows = positions.shape[1] * 8
    return (
        beta_real.reshape(rows, -1).astype(jnp.bfloat16),
        beta_imag.reshape(rows, -1).astype(jnp.bfloat16),
    )


def project(beta_real, beta_imag, wave_real, wave_imag):
    proj_real = jnp.dot(beta_real, wave_real, preferred_element_type=jnp.float32) + jnp.dot(
        beta_imag, wave_imag, preferred_element_type=jnp.float32
    )
    proj_imag = jnp.dot(beta_real, wave_imag, preferred_element_type=jnp.float32) - jnp.dot(
        beta_imag, wave_real, preferred_element_type=jnp.float32
    )
    return jnp.stack([proj_real, proj_imag], axis=1)


def occupancy_terms(projections, weights):
    grouped = projections.reshape(projections.shape[0] // 8, 8, 2, projections.shape[2])
    return jnp.einsum("aicn,ajcn,n->aij", grouped, grouped, weights, precision=HIGH)


def onsite_matrix(occupancy, atom_species, onsite_base, coupling):
    holding = occupancy.shape[0]
    kinds = onsite_base.shape[0]
    onehot = (atom_species[:, None] == jnp.arange(kinds, dtype=jnp.int32)[None, :]).astype(
        jnp.float32
    )
    response = jnp.einsum("skl,al->ask", coupling, occupancy.reshape(holding, 64), precision=HIGH)
    base = jnp.einsum("as,sk->ak", onehot, onsite_base.reshape(kinds, 64), precision=HIGH)
    total = base + jnp.einsum("as,ask->ak", onehot, response, precision=HIGH)
    return total.reshape(holding, 8, 8)


def weigh(onsite, projections):
    grouped = projections.reshape(projections.shape[0] // 8, 8, 2, projections.shape[2])
    weighted = jnp.einsum("aij,ajcn->aicn", onsite, grouped, precision=HIGH)
    return weighted.reshape(projections.shape).astype(jnp.bfloat16)


def back_project(beta_real, beta_imag, weighted):
    dims = (((0,), (0,)), ((), ()))
    q_real = weighted[:, 0, :]
    q_imag = weighted[:, 1, :]
    out_real = lax.dot_general(
        beta_real, q_real, dims, preferred_element_type=jnp.float32
    ) - lax.dot_general(beta_imag, q_imag, dims, preferred_element_type=jnp.float32)
    out_imag = lax.dot_general(
        beta_real, q_imag, dims, preferred_element_type=jnp.float32
    ) + lax.dot_general(beta_imag, q_real, dims, preferred_element_type=jnp.float32)
    return jnp.stack([out_real, out_imag], axis=0)


def local(
    wavefunctions,
    miller,
    reciprocal,
    fractional,
    species,
    atom_order,
    radial_widths,
    onsite_base,
    coupling,
    occupations,
):
    sorted_species = species[atom_order]
    sorted_positions = fractional[:, atom_order]
    owned_atoms = atom_order.shape[0] // lax.axis_size("pw")
    owner_index = lax.axis_index("pw")
    weights = occupations / (occupations.shape[0] * lax.axis_size("band"))
    wave_real = wavefunctions[0]
    wave_imag = wavefunctions[1]
    positions = sorted_positions
    kinds = sorted_species
    beta_real, beta_imag = projector_tile(miller, reciprocal, positions, kinds, radial_widths)
    projections = lax.psum_scatter(
        project(beta_real, beta_imag, wave_real, wave_imag), "pw", scatter_dimension=0, tiled=True
    )
    own_species = lax.dynamic_slice_in_dim(
        sorted_species, owner_index * owned_atoms, owned_atoms, 0
    )
    occupancy = lax.psum(occupancy_terms(projections, weights), "band")
    onsite_own = onsite_matrix(occupancy, own_species, onsite_base, coupling)
    weighted = weigh(onsite_own, projections)
    positions = sorted_positions
    kinds = sorted_species
    beta_real, beta_imag = projector_tile(miller, reciprocal, positions, kinds, radial_widths)
    applied = back_project(beta_real, beta_imag, lax.all_gather(weighted, "pw", axis=0, tiled=True))
    return (applied.astype(jnp.bfloat16), onsite_own)


def solution(mesh):
    placed = (P(None, "pw", "band"), P(None, "pw"), P(), P(), P(), P(), P(), P(), P(), P("band"))
    return jax.shard_map(
        local,
        mesh=mesh,
        in_specs=placed,
        out_specs=(P(None, "pw", "band"), P("pw", None, None)),
        check_vma=False,
    )
```

profile of v0, /device:TPU:0, one launch (start us, length us, event | category | flops | bytes accessed | tf_op | source)
XLA Modules:
  0.0 84.7 jit_solution(17103418098538546727)
XLA Ops:
  7.2 0.0 copy-start
  7.2 0.0 reduce-scatter.2.cloned.1.call-start
  7.2 0.7 compare_select_fusion
  7.9 0.6 copy-done.1
  8.6 0.7 gather_fusion
  9.3 0.0 copy-start.4
  9.3 0.2 fusion.36
  9.5 0.5 copy-done.4
  10.0 0.2 copy-done.6
  10.2 0.2 multiply_reduce_fusion
  10.4 0.1 copy.17
  10.5 0.6 copy-done.7
  11.0 0.1 copy.18
  11.1 0.6 gather_fusion.1
  11.7 0.4 fusion.35
  12.1 0.1 multiply_exponential_fusion
  12.3 0.2 slice_multiply_fusion.1
  12.5 0.1 multiply_convert_fusion.2
  12.6 0.1 broadcast_multiply_fusion.1
  12.7 0.2 multiply_convert_fusion
  12.9 0.8 copy-done.3
  13.7 0.3 fusion.6
  13.9 0.3 fusion.10
  14.2 0.3 fusion.4
  14.5 0.3 fusion.5
  14.7 0.7 pad_maximum_fusion
  15.5 0.0 reduce-scatter.2.cloned.1.call-update
  15.5 0.7 copy-done.5
  16.2 0.1 reshape.77
  16.3 0.1 dynamic_slice.3
  16.3 0.6 copy-done.9
  16.9 0.1 fusion.33
  17.0 32.1 %reduce-scatter.2.cloned.1.call-done = f32[32,2,128]{2,0,1:T(8,128)} async-done(((f32[256,2,128]{2,0,1:T(8,128)}), f32[32,2,128]{2,0,1:T(8,128)}) %reduce-scatter.2.cloned.1.call-update) | async-done | bytes 32784 | tf_op jit(solution)/shard_map/reduce_scatter | solution.py:104
  49.1 1.0 %convolution_bitcast_fusion = f32[4,8,8]{2,1,0:T(8,128)S(1)} fusion(f32[128]{0:T(128)S(1)} %broadcast_multiply_fusion.3, f32[32,2,128]{2,0,1:T(8,128)} %reduce-scatter.2.cloned.1.call-done), kind=kOutput, calls=%fused_computation.14 | convolution fusion | flops 794624 | bytes 34304 | tf_op jit(solution)/shard_map/aicn,ajcn,n->aij/dot_general | solution.py:48
  50.1 0.1 reshape.79
  50.2 9.9 %psum.7 = f32[4,64]{1,0:T(4,128)S(1)} all-reduce(f32[4,64]{1,0:T(4,128)S(1)} %reshape.79), channel_id=1, replica_groups=mesh['pw'=8,'band'=4] {'band'}, use_global_device_ids=true, to_apply=%region_2.0 | all-reduce | flops 256 | bytes 2048 | tf_op jit(solution)/shard_map/psum | solution.py:110
  60.1 0.4 fusion.31
  60.5 0.2 fusion.28
  60.6 0.2 convolution_add_fusion.2
  60.8 0.1 reshape.103
  60.9 0.7 reshape.80
  61.6 0.2 convolution_convert_fusion
  61.8 14.0 %all_gather.3 = bf16[256,2,128]{2,0,1:T(8,128)(2,1)S(1)} all-gather(bf16[32,2,128]{2,0,1:T(8,128)(2,1)S(1)} %bitcast.79), channel_id=1, replica_groups=mesh['pw'=8,'band'=4] {'pw'}, dimensions={0}, use_global_device_ids=true | all-gather | bytes 147456 | tf_op jit(solution)/shard_map/all_gather | solution.py:116
  75.8 0.3 fusion.17
  76.1 0.3 fusion.16
  76.4 0.3 fusion.2
  76.8 0.3 fusion.3
  77.1 0.7 pad_maximum_fusion.1
  (17 shorter events, 0.1 us)
Async XLA Ops:
  7.2 52.9 %copy-start = (f32[4,64,64]{2,1,0:T(8,128)S(1)}, f32[4,64,64]{2,1,0:T(8,128)}, u32[]{:S(2)}) copy-start(f32[4,64,64]{2,1,0:T(8,128)} %param.18) | copy-start | bytes 196612
  7.2 42.0 %reduce-scatter.2.cloned.1.call-start = ((), (), s32[]{:S(2)}) async-start(), calls=%async_computation.1 | async-start | bytes 294912 | tf_op jit(solution)/shard_map/reduce_scatter | solution.py:104
  7.9 0.7 copy-start.1
  8.6 0.7 copy-start.8
  9.3 0.7 copy-start.4
  9.5 0.7 copy-start.6
  10.4 0.7 copy-start.7
  12.7 1.0 %copy-start.3 = (bf16[2,512,128]{2,1,0:T(8,128)(2,1)S(1)}, bf16[2,512,128]{2,1,0:T(8,128)(2,1)}, u32[]{:S(2)}) copy-start(bf16[2,512,128]{2,1,0:T(8,128)(2,1)} %param.10) | copy-start | bytes 786436
  15.5 0.7 copy-start.5
  16.3 0.7 copy-start.9
  60.8 0.8 copy-start.2
Sparse Core Ops, SparseCore 0:
  15.6 33.4 reduce-scatter.1
where the time goes:
time: 85.2 us; the launch traced here: 84.7 us
  waiting for transfers between devices  32.2 us (38%)
  blocking collectives  23.8 us (28%)
  between operations  14.2 us (17%)
  local copies, waits for them, and re-layouts  6.47 us (8%)
  matrix products  5.02 us (6%)
  other arithmetic  2.96 us (3%)
    reduce_scatter x1, waiting for transfers between devices, local(): lax.psum_scatter(project(beta_real, beta_imag, wave_real, wave_imag), 'pw...  32.1 us
    all_gather x1, blocking collectives, local(): lax.all_gather(weighted, 'pw', axis=0, tiled=True)  14 us
    psum x1, blocking collectives, local(): occupancy = lax.psum(occupancy_terms(projections, weights), 'band')  9.88 us
    unnamed x22, local copies, waits for them, and re-layouts  4.07 us
  transfers between devices with their start and end apart: 1, of which 1 were waited for; matrix products, arithmetic and copies ran while one was open for 0% of the time, Pallas kernels for 0%

commit v1 on v0

--- a/solution.py
+++ b/solution.py
@@ -113,7 +113,13 @@
     positions = sorted_positions
     kinds = sorted_species
     beta_real, beta_imag = projector_tile(miller, reciprocal, positions, kinds, radial_widths)
-    applied = back_project(beta_real, beta_imag, lax.all_gather(weighted, "pw", axis=0, tiled=True))
+    applied = back_project(
+        beta_real,
+        beta_imag,
+        jnp.concatenate(
+            lax.all_to_all(jnp.stack([weighted] * lax.axis_size("pw")), "pw", 0, 0), axis=0
+        ),
+    )
     return (applied.astype(jnp.bfloat16), onsite_own)
 
 

time: 85.2 us -> 81.9 us (0.961)
  blocking collectives: 23.8 us -> 9.88 us
  waiting for transfers between devices: 32.2 us -> 38.2 us
  starting transfers between devices: 0.04 us -> 3.41 us
  local copies, waits for them, and re-layouts: 6.47 us -> 7.63 us
    all_gather x1 -> x0, blocking collectives: 14 us -> none  [local(): lax.all_gather(weighted, 'pw', axis=0, tiled=True)]
    all_to_all x0 -> x1, waiting for transfers between devices: none -> 6 us  [local(): lax.all_to_all(jnp.stack([weighted] * lax.axis_size('pw')), 'pw', 0, 0)]
    all_to_all x0 -> x1, starting transfers between devices: none -> 3.37 us  [local(): lax.all_to_all(jnp.stack([weighted] * lax.axis_size('pw')), 'pw', 0, 0)]
  transfers between devices with their start and end apart: 1 -> 2, of which waited for: 1 -> 2; matrix products, arithmetic and copies ran while one was open for 0% -> 1% of each run, Pallas kernels for 0% -> 0%
where the time goes in v1:
time: 81.9 us; the launch traced here: 81.3 us
  waiting for transfers between devices  38.2 us (47%)
  between operations  14.2 us (17%)
  blocking collectives  9.88 us (12%)
  local copies, waits for them, and re-layouts  7.63 us (9%)
  matrix products  5.03 us (6%)
  starting transfers between devices  3.41 us (4%)
  other arithmetic  2.95 us (4%)
    reduce_scatter x1, waiting for transfers between devices, local(): lax.psum_scatter(project(beta_real, beta_imag, wave_real, wave_imag), 'pw...  32.1 us
    psum x1, blocking collectives, local(): occupancy = lax.psum(occupancy_terms(projections, weights), 'band')  9.88 us
    all_to_all x1, waiting for transfers between devices, local(): lax.all_to_all(jnp.stack([weighted] * lax.axis_size('pw')), 'pw', 0, 0)  6 us
    unnamed x22, local copies, waits for them, and re-layouts  4.56 us
    all_to_all x1, starting transfers between devices, local(): lax.all_to_all(jnp.stack([weighted] * lax.axis_size('pw')), 'pw', 0, 0)  3.37 us
  transfers between devices with their start and end apart: 2, of which 2 were waited for; matrix products, arithmetic and copies ran while one was open for 1% of the time, Pallas kernels for 0%

profile of v1, /device:TPU:0, one launch (start us, length us, event | category | flops | bytes accessed | tf_op | source)
XLA Modules:
  0.0 81.3 jit_solution(5538594120152261430)
XLA Ops:
  7.2 0.0 reduce-scatter.2.cloned.1.call-start
  7.2 0.7 compare_select_fusion
  7.9 0.6 copy-done.1
  8.6 0.7 gather_fusion
  9.3 0.2 fusion.36
  9.5 0.5 copy-done.4
  10.0 0.2 copy-done.6
  10.2 0.2 multiply_reduce_fusion
  10.4 0.1 copy.23
  10.5 0.6 copy-done.7
  11.0 0.1 copy.24
  11.1 0.6 gather_fusion.1
  11.7 0.4 fusion.35
  12.1 0.1 multiply_exponential_fusion
  12.3 0.2 slice_multiply_fusion.1
  12.5 0.1 multiply_convert_fusion.2
  12.6 0.1 broadcast_multiply_fusion.1
  12.7 0.2 multiply_convert_fusion
  12.9 0.8 copy-done.3
  13.7 0.3 fusion.6
  13.9 0.3 fusion.10
  14.2 0.3 fusion.4
  14.5 0.3 fusion.5
  14.7 0.7 pad_maximum_fusion
  15.5 0.7 copy-done.5
  16.2 0.1 reshape.83
  16.3 0.1 dynamic_slice.3
  16.3 0.6 copy-done.9
  16.9 0.1 fusion.33
  17.0 32.1 %reduce-scatter.2.cloned.1.call-done = f32[32,2,128]{2,0,1:T(8,128)} async-done(((f32[256,2,128]{2,0,1:T(8,128)}), f32[32,2,128]{2,0,1:T(8,128)}) %reduce-scatter.2.cloned.1.call-update) | async-done | bytes 32784 | tf_op jit(solution)/shard_map/reduce_scatter | solution.py:104
  49.1 1.0 %convolution_bitcast_fusion = f32[4,8,8]{2,1,0:T(8,128)S(1)} fusion(f32[128]{0:T(128)S(1)} %broadcast_multiply_fusion.3, f32[32,2,128]{2,0,1:T(8,128)} %reduce-scatter.2.cloned.1.call-done), kind=kOutput, calls=%fused_computation.14 | convolution fusion | flops 794624 | bytes 34304 | tf_op jit(solution)/shard_map/aicn,ajcn,n->aij/dot_general | solution.py:48
  50.1 0.1 reshape.85
  50.2 9.9 %psum.7 = f32[4,64]{1,0:T(4,128)S(1)} all-reduce(f32[4,64]{1,0:T(4,128)S(1)} %reshape.85), channel_id=1, replica_groups=mesh['pw'=8,'band'=4] {'band'}, use_global_device_ids=true, to_apply=%region_2.0 | all-reduce | flops 256 | bytes 2048 | tf_op jit(solution)/shard_map/psum | solution.py:110
  60.1 0.4 fusion.31
  60.5 0.2 fusion.28
  60.6 0.2 convolution_add_fusion.2
  60.8 0.1 reshape.110
  60.9 0.5 copy-done.2
  61.4 0.2 convolution_convert_fusion
  61.6 0.7 stack.35
  62.3 3.4 %all-to-all-start = ((bf16[8,32,2,128]{3,1,2,0:T(8,128)(2,1)}), bf16[8,32,2,128]{3,1,2,0:T(8,128)(2,1)S(1)}, u32[]{:S(2)}, u32[]{:S(2)}) async-start(bf16[8,32,2,128]{3,1,2,0:T(8,128)(2,1)} %stack.35), calls=%async_computation.1 | async-start | bytes 262144 | tf_op jit(solution)/shard_map/all_to_all | solution.py:120
  65.6 0.7 reshape.86
  66.3 6.0 %all-to-all-done = bf16[8,32,2,128]{3,1,2,0:T(8,128)(2,1)S(1)} async-done(((bf16[8,32,2,128]{3,1,2,0:T(8,128)(2,1)}), bf16[8,32,2,128]{3,1,2,0:T(8,128)(2,1)S(1)}, u32[]{:S(2)}, u32[]{:S(2)}) %all-to-all-start) | async-done | bytes 131104 | tf_op jit(solution)/shard_map/all_to_all | solution.py:120
  72.3 0.3 fusion.17
  72.7 0.3 fusion.16
  73.0 0.3 fusion.2
  73.4 0.3 fusion.3
  73.7 0.7 pad_maximum_fusion.1
  (20 shorter events, 0.1 us)
Async XLA Ops:
  7.2 52.9 %copy-start = (f32[4,64,64]{2,1,0:T(8,128)S(1)}, f32[4,64,64]{2,1,0:T(8,128)}, u32[]{:S(2)}) copy-start(f32[4,64,64]{2,1,0:T(8,128)} %param.18) | copy-start | bytes 196612
  7.2 41.9 %reduce-scatter.2.cloned.1.call-start = ((), (), s32[]{:S(2)}) async-start(), calls=%async_computation.2 | async-start | bytes 294912 | tf_op jit(solution)/shard_map/reduce_scatter | solution.py:104
  7.9 0.7 copy-start.1
  8.6 0.7 copy-start.8
  9.3 0.7 copy-start.4
  9.5 0.7 copy-start.6
  10.4 0.7 copy-start.7
  12.7 1.0 %copy-start.3 = (bf16[2,512,128]{2,1,0:T(8,128)(2,1)S(1)}, bf16[2,512,128]{2,1,0:T(8,128)(2,1)}, u32[]{:S(2)}) copy-start(bf16[2,512,128]{2,1,0:T(8,128)(2,1)} %param.10) | copy-start | bytes 786436
  15.5 0.7 copy-start.5
  16.3 0.7 copy-start.9
  60.6 0.8 copy-start.2
  62.3 10.1 %all-to-all-start = ((bf16[8,32,2,128]{3,1,2,0:T(8,128)(2,1)}), bf16[8,32,2,128]{3,1,2,0:T(8,128)(2,1)S(1)}, u32[]{:S(2)}, u32[]{:S(2)}) async-start(bf16[8,32,2,128]{3,1,2,0:T(8,128)(2,1)} %stack.35), calls=%async_computation.1 | async-start | bytes 262144 | tf_op jit(solution)/shard_map/all_to_all | solution.py:120
Sparse Core Ops, SparseCore 0:
  15.6 33.4 reduce-scatter.1
